TPU v7x, 8 devices: a whole 2x2x1 slice. The times are simulated.
8 devices in a mesh: dp: 2 (over y, z), ep: 4 (over x, core).
Axes of the slice: x: 2, y: 2, z: 1, core: 2. Of those that a mesh axis runs over, the one named last changes fastest.
Arguments:
- x: bfloat16 [2, 4, 768, 2048], P('dp', 'ep'), parts along dimension 0
- expert: int32 [2, 4, 768, 6], P('dp', 'ep'), parts along dimension 0
- slot: int32 [2, 4, 768, 6], P('dp', 'ep'), parts along dimension 0
- gate: float32 [2, 4, 768, 6], P('dp', 'ep'), parts along dimension 0
- w_gate: bfloat16 [64, 2048, 1408], P('ep')
- w_up: bfloat16 [64, 2048, 1408], P('ep')
- w_down: bfloat16 [64, 1408, 2048], P('ep')
- s_gate: bfloat16 [2048, 2816], replicated
- s_up: bfloat16 [2048, 2816], replicated
- s_down: bfloat16 [2816, 2048], replicated
Outputs:
- y: bfloat16 [2, 4, 768, 2048], P('dp', 'ep'), parts along dimension 0
There are 2 independent parts. A program takes and returns all parts, laid end to end along the dimension named above; an argument that names none is the same for every part.
All inputs are finite; a program needn't handle non-finite values.
Results may differ from a plain program's by a relative error of at most 0.009.
Values are sent between devices in bfloat16 or wider.
A program may use at most 2 GiB of HBM per device.

v0:
```python
import jax
import jax.numpy as jnp
from jax import lax
from jax.sharding import NamedSharding, PartitionSpec as P


def einsum(form, a, b):
    return jnp.einsum(form, a.astype(jnp.float32), b.astype(jnp.float32))


def for_all(x, s_gate, s_up, s_down):
    h = jax.nn.silu(einsum("...d,df->...f", x, s_gate)) * einsum("...d,df->...f", x, s_up)
    return einsum("...f,fd->...d", h.astype(jnp.bfloat16), s_down)


def solution(mesh):
    def placed(v, *spec):
        return lax.with_sharding_constraint(v, NamedSharding(mesh, P(*spec)))

    def step(x, expert, slot, gate, w_gate, w_up, w_down, s_gate, s_up, s_down):
        experts, (tokens, top) = w_gate.shape[0], expert.shape[2:]
        slots = 5 * tokens * top // (4 * experts)
        to_expert = jax.nn.one_hot(expert, experts, dtype=jnp.bfloat16)
        to_slot = jax.nn.one_hot(slot, slots, dtype=jnp.bfloat16)
        weighted = to_expert * gate[..., None].astype(jnp.bfloat16)
        dispatch = einsum("abtke,abtkc->abtec", to_expert, to_slot).astype(jnp.bfloat16)
        combine = einsum("abtke,abtkc->abtec", weighted, to_slot).astype(jnp.bfloat16)
        z = einsum("abtec,abtd->aebcd", dispatch, x).astype(jnp.bfloat16)
        z = placed(z, "dp", None, "ep", None, None)
        z = placed(z, "dp", "ep", None, None, None)
        h = jax.nn.silu(einsum("aebcd,edf->aebcf", z, w_gate))
        h = (h * einsum("aebcd,edf->aebcf", z, w_up)).astype(jnp.bfloat16)
        out = einsum("aebcf,efd->aebcd", h, w_down).astype(jnp.bfloat16)
        out = placed(out, "dp", "ep", None, None, None)
        out = placed(out, "dp", None, "ep", None, None)
        y = einsum("abtec,aebcd->abtd", combine, out)
        return (y + for_all(x, s_gate, s_up, s_down)).astype(jnp.bfloat16)

    return step
```

profile of v0, /device:TPU:0, one launch (start us, length us, event | category | flops | bytes accessed | tf_op | source)
XLA Modules:
  0.0 1075.1 jit_solution(11245192725656225449)
XLA Ops:
  0.0 0.0 copy-start
  0.0 1.0 copy.25
  1.1 0.0 copy-start.2
  1.1 1.7 copy.27
  2.7 11.9 %convolution_convert_fusion.1 = bf16[768,64,90]{2,1,0:T(8,128)(2,1)S(1)} fusion(s32[768,6]{1,0:T(8,128)} %bitcast.123, s32[768,6]{1,0:T(8,128)S(1)} %bitcast.121), kind=kOutput, calls=%fused_computation.28 | convolution fusion | flops 58217472 | bytes 8884224 | tf_op jit(solution)/abtke,abtkc->abtec/dot_general | solution.py:8
  14.7 0.0 copy-done
  14.7 47.5 %convolution_convert_fusion = bf16[64,90,2048]{2,1,0:T(8,128)(2,1)} fusion(bf16[768,64,90]{2,1,0:T(8,128)(2,1)S(1)} %convolution_convert_fusion.1, bf16[1,1,768,2048]{3,2,1,0:T(8,128)(2,1)S(1)} %copy-done), kind=kOutput, calls=%fused_computation.19 | convolution fusion | flops 18131189760 | bytes 35586048 | tf_op jit(solution)/abtec,abtd->aebcd/dot_general | solution.py:8
  62.2 0.0 copy-done.2
  62.2 22.2 %copy.14 = bf16[1,4,16,1,90,2048]{5,2,4,3,0,1:T(8,128)(2,1)S(1)} copy(bf16[1,4,16,1,90,2048]{5,4,2,1,3,0:T(8,128)(2,1)} %bitcast.119) | data formatting | bytes 47185920 | tf_op jit(solution)/sharding_constraint;jit(solution)/sharding_constraint | solution.py:18
  84.4 261.9 %all-to-all.4 = bf16[1,4,16,1,90,2048]{5,2,4,3,0,1:T(8,128)(2,1)} all-to-all(bf16[1,4,16,1,90,2048]{5,2,4,3,0,1:T(8,128)(2,1)S(1)} %copy.14), channel_id=1, replica_groups=mesh['dp'=2,'ep'=4] {'ep'}, dimensions={1} | all-to-all | bytes 47185920 | tf_op jit(solution)/sharding_constraint;jit(solution)/sharding_constraint | solution.py:18
  346.3 121.7 %fusion.2 = f32[16,4,90,1408]{3,2,1,0:T(8,128)} fusion(bf16[16,2048,1408]{2,1,0:T(8,128)(2,1)} %param.5, bf16[1,4,16,1,90,2048]{5,2,4,3,0,1:T(8,128)(2,1)} %all-to-all.4), kind=kOutput, calls=%fused_computation.2 | convolution fusion | flops 33218887680 | bytes 148307968 | tf_op jit(solution)/aebcd,edf->aebcf/dot_general | solution.py:8
  468.1 216.6 %fusion.6 = bf16[1,16,4,90,1408]{4,3,2,1,0:T(8,128)(2,1)} fusion(f32[16,4,90,1408]{3,2,1,0:T(8,128)} %fusion.2, bf16[16,2048,1408]{2,1,0:T(8,128)(2,1)} %param.4, bf16[1,4,16,1,90,2048]{5,2,4,3,0,1:T(8,128)(2,1)} %all-to-all.4), kind=kOutput, calls=%fused_computation.7 | convolution fusion | flops 33267548160 | bytes 164528128 | tf_op jit(solution)/aebcd,edf->aebcf/dot_general | solution.py:8
  684.7 53.8 %convert_bitcast_fusion = bf16[1,16,4,1,90,2048]{5,4,2,1,3,0:T(8,128)(2,1)} fusion(bf16[16,1408,2048]{2,1,0:T(8,128)(2,1)} %param.6, bf16[1,16,4,90,1408]{4,3,2,1,0:T(8,128)(2,1)} %fusion.6), kind=kOutput, calls=%fused_computation.15 | convolution fusion | flops 33230684160 | bytes 132087808 | tf_op jit(solution)/aebcf,efd->aebcd/dot_general | solution.py:8
  738.5 26.3 %copy.16 = bf16[1,16,4,1,90,2048]{5,1,4,3,0,2:T(8,128)(2,1)} copy(bf16[1,16,4,1,90,2048]{5,4,2,1,3,0:T(8,128)(2,1)} %convert_bitcast_fusion) | data formatting | bytes 47185920 | tf_op jit(solution)/sharding_constraint;jit(solution)/sharding_constraint | solution.py:18
  764.9 8.3 all-to-all-start.1
  773.2 1.3 convert_element_type.75
  774.5 1.6 copy.26
  776.1 14.3 %convolution_convert_fusion.2 = bf16[768,64,90]{2,1,0:T(8,128)(2,1)} fusion(s32[768,6]{1,0:T(8,128)} %bitcast.124, s32[768,6]{1,0:T(8,128)S(1)} %bitcast.122, bf16[768,6]{1,0:T(8,128)(2,1)} %bitcast.125), kind=kOutput, calls=%fused_computation.29 | convolution fusion | flops 58512384 | bytes 8893440 | tf_op jit(solution)/abtke,abtkc->abtec/dot_general | solution.py:8
  790.5 17.6 %copy.23 = bf16[768,64,90]{0,1,2:T(8,128)(2,1)} copy(bf16[768,64,90]{2,1,0:T(8,128)(2,1)} %convolution_convert_fusion.2) | data formatting | bytes 17694720 | tf_op jit(solution)/convert_element_type | solution.py:27
  808.1 15.0 %fusion.31 = f32[768,2816]{1,0:T(8,128)} fusion(bf16[2048,2816]{1,0:T(8,128)(2,1)} %param.7, bf16[1,1,768,2048]{3,2,1,0:T(8,128)(2,1)S(1)} %copy-done), kind=kOutput, calls=%fused_computation.36 | convolution fusion | flops 8858370048 | bytes 23330816 | tf_op jit(solution)/...d,df->...f/dot_general | solution.py:8
  823.1 31.0 %fusion.28 = f32[768,2048]{1,0:T(8,128)} fusion(bf16[2816,2048]{1,0:T(8,128)(2,1)} %param.9, bf16[2048,2816]{1,0:T(8,128)(2,1)} %param.8, f32[768,2816]{1,0:T(8,128)} %fusion.31, bf16[1,1,768,2048]{3,2,1,0:T(8,128)(2,1)S(1)} %copy-done), kind=kOutput, calls=%fused_computation.33 | convolution fusion | flops 17729716224 | bytes 41156608 | tf_op jit(solution)/...f,fd->...d/dot_general | solution.py:8
  854.1 174.8 %all-to-all-done.1 = bf16[1,16,4,1,90,2048]{5,1,4,3,0,2:T(8,128)(2,1)} async-done(((bf16[1,16,4,1,90,2048]{5,1,4,3,0,2:T(8,128)(2,1)}), bf16[1,16,4,1,90,2048]{5,1,4,3,0,2:T(8,128)(2,1)}, u32[]{:S(2)}, u32[]{:S(2)}) %all-to-all-start.1) | async-done | bytes 23592992 | tf_op jit(solution)/sharding_constraint;jit(solution)/sharding_constraint | solution.py:18
  1028.9 22.5 %copy.17 = bf16[1,16,4,1,90,2048]{5,1,2,4,3,0:T(8,128)(2,1)} copy(bf16[1,16,4,1,90,2048]{5,1,4,3,0,2:T(8,128)(2,1)} %all-to-all-done.1) | data formatting | bytes 47185920 | tf_op jit(solution)/sharding_constraint;jit(solution)/sharding_constraint | solution.py:18
  1051.4 23.2 %fusion.41 = bf16[1,1,768,2048]{3,2,1,0:T(8,128)(2,1)} fusion(f32[768,2048]{1,0:T(8,128)S(1)} %copy-done.4, bf16[768,64,90]{0,1,2:T(8,128)(2,1)S(1)} %copy-done.1, bf16[64,90,2048]{2,0,1:T(8,128)(2,1)} %bitcast.120), kind=kOutput, calls=%fused_computation.44 | convolution fusion | flops 18122539008 | bytes 41877504 | tf_op jit(solution)/abtec,aebcd->abtd/dot_general | solution.py:8
  (6 shorter events, 0.0 us)
Async XLA Ops:
  0.0 14.7 %copy-start = (bf16[1,1,768,2048]{3,2,1,0:T(8,128)(2,1)S(1)}, bf16[1,1,768,2048]{3,2,1,0:T(8,128)(2,1)}, u32[]{:S(2)}) copy-start(bf16[1,1,768,2048]{3,2,1,0:T(8,128)(2,1)} %param.3) | copy-start | bytes 9437188
  1.1 61.1 %copy-start.2 = (s32[1,1,768,6]{3,2,1,0:T(8,128)}, s32[1,1,768,6]{3,2,1,0:T(8,128)S(1)}, u32[]{:S(2)}) copy-start(s32[1,1,768,6]{3,2,1,0:T(8,128)S(1)} %copy.25) | copy-start | bytes 55300
  764.9 11.2 %copy-start.3 = (s32[1,1,768,6]{3,2,1,0:T(8,128)S(1)}, s32[1,1,768,6]{3,2,1,0:T(8,128)}, u32[]{:S(2)}) copy-start(s32[1,1,768,6]{3,2,1,0:T(8,128)} %copy-done.2) | copy-start | bytes 55300
  764.9 264.0 %all-to-all-start.1 = ((bf16[1,16,4,1,90,2048]{5,1,4,3,0,2:T(8,128)(2,1)}), bf16[1,16,4,1,90,2048]{5,1,4,3,0,2:T(8,128)(2,1)}, u32[]{:S(2)}, u32[]{:S(2)}) async-start(bf16[1,16,4,1,90,2048]{5,1,4,3,0,2:T(8,128)(2,1)} %copy.16), calls=%async_computation.1 | async-start | bytes 47185920 | tf_op jit(solution)/sharding_constraint;jit(solution)/sharding_constraint | solution.py:18
  1028.9 22.5 %copy-start.1 = (bf16[768,64,90]{0,1,2:T(8,128)(2,1)S(1)}, bf16[768,64,90]{0,1,2:T(8,128)(2,1)}, u32[]{:S(2)}) copy-start(bf16[768,64,90]{0,1,2:T(8,128)(2,1)} %copy.23) | copy-start | bytes 26542084
  1028.9 22.5 %copy-start.4 = (f32[768,2048]{1,0:T(8,128)S(1)}, f32[768,2048]{1,0:T(8,128)}, u32[]{:S(2)}) copy-start(f32[768,2048]{1,0:T(8,128)} %fusion.28) | copy-start | bytes 18874372
where the time goes:
time: 1090 us; the launch traced here: 1080 us
  matrix products  535 us (49%)
  blocking collectives  262 us (24%)
  waiting for transfers between devices  175 us (16%)
  local copies, waits for them, and re-layouts  93 us (9%)
    dot_general x9, matrix products, einsum(): return jnp.einsum(form, a.astype(jnp.float32), b.astype(jnp.float32))  535 us
    another operation x1, blocking collectives, placed(): return lax.with_sharding_constraint(v, NamedSharding(mesh, P(*spec)))  262 us
    another operation x1, waiting for transfers between devices, placed(): return lax.with_sharding_constraint(v, NamedSharding(mesh, P(*spec)))  175 us
    another operation x3, local copies, waits for them, and re-layouts, placed(): return lax.with_sharding_constraint(v, NamedSharding(mesh, P(*spec)))  71 us
  transfers between devices with their start and end apart: 1, of which 1 were waited for; matrix products, arithmetic and copies ran while one was open for 8% of the time, Pallas kernels for 0%

commit v1 on v0

v1 whole, which is shorter than its diff:
```python
import functools

import jax
import jax.numpy as jnp
from jax import lax
from jax.experimental import pallas as pl
from jax.experimental.pallas import tpu as pltpu
from jax.sharding import PartitionSpec as P


F32, BF16, I32 = jnp.float32, jnp.bfloat16, jnp.int32
VMEM = 66_000_000
GROUP, BLOCK, STRIDE, PIECE, TILE = 16, 256, 128, 32, 128
CHUNKS = 4


def dot(a, b):
    return jnp.dot(a, b, preferred_element_type=F32)


def params():
    return pltpu.CompilerParams(vmem_limit_bytes=VMEM)


def cost(flops, nbytes):
    return pl.CostEstimate(flops=int(flops), bytes_accessed=int(nbytes), transcendentals=0)


def whole(v):
    return pl.BlockSpec(v.shape, lambda *_: (0,) * v.ndim, pipeline_mode=pl.Buffered(1))


def aligned(v, m=GROUP):
    return pl.multiple_of(v, m)


def route_kernel(local, me_ref, *refs):
    infos, (pos_ref, table_ref) = refs[:4], refs[4:]
    top, tokens = pos_ref.shape[1:]
    expert = lax.broadcasted_iota(I32, (local, tokens), 0)
    a = lax.broadcasted_iota(I32, (local, STRIDE), 0)
    b = lax.broadcasted_iota(I32, (local, STRIDE), 1)
    for s, info in enumerate(infos):
        code = info[:top, :].astype(I32) - me_ref[0] * (local * STRIDE)
        mine = (code >= 0) & (code < local * STRIDE)
        which = jnp.where(mine, lax.shift_right_logical(code, 7), -1)
        place = jnp.where(mine, code & (STRIDE - 1), 0)
        most = jnp.zeros((local, tokens), I32)
        for j in range(top):
            most = jnp.maximum(most, jnp.where(which[j : j + 1] == expert, place[j : j + 1] + 1, 0))
        used = jnp.max(most.astype(F32), axis=1, keepdims=True).astype(I32)
        used = (used + (GROUP - 1)) & ~(GROUP - 1)
        as_row = lambda m: jnp.sum(jnp.where(m, used.astype(F32), 0.0), axis=0, keepdims=True)
        row, start_row = as_row(a == b), as_row(a < b)
        start = jnp.sum(jnp.where((b < a) & (b < local), row, 0.0), axis=1, keepdims=True).astype(I32)
        for j in range(top):
            at = jnp.sum(jnp.where(which[j : j + 1] == expert, start, 0).astype(F32), axis=0, keepdims=True).astype(I32)
            pos_ref[s, j : j + 1, :] = jnp.where(mine[j : j + 1], at + place[j : j + 1], -1)
        table_ref[s : s + 1, :] = row.astype(I32)
        table_ref[4 + s : 5 + s, :] = start_row.astype(I32)


def route(me, infos, local, top):
    tokens = infos[0].shape[1]
    return pl.pallas_call(
        functools.partial(route_kernel, local),
        in_specs=[pl.BlockSpec(memory_space=pltpu.SMEM)] + [pl.BlockSpec(memory_space=pltpu.VMEM)] * 4,
        out_specs=[pl.BlockSpec(memory_space=pltpu.VMEM)] * 2,
        out_shape=[jax.ShapeDtypeStruct((4, top, tokens), I32), jax.ShapeDtypeStruct((8, STRIDE), I32)],
        cost_estimate=cost(1e9, 1e6),
        name="route",
    )(me, *infos)


def gather_kernel(s, local, table_ref, pos_ref, info_ref, x_ref, z_ref, c_ref):
    i, (top, tokens) = pl.program_id(0), pos_ref.shape[1:]

    @pl.when(i * BLOCK < table_ref[4 + s, local])
    def _():
        row = lax.broadcasted_iota(I32, (BLOCK, tokens), 0) + i * BLOCK
        c, one = jnp.zeros((BLOCK, tokens), F32), jnp.zeros((BLOCK, tokens), F32)
        for j in range(top):
            hit = pos_ref[s, j : j + 1, :] == row
            c = jnp.where(hit, info_ref[top + j : top + j + 1, :], c)
            one = jnp.where(hit, 1.0, one)
        z_ref[...] = dot(one.astype(BF16), x_ref[...]).astype(BF16)
        c_ref[...] = c.T.astype(BF16)


def gather(table, pos, info, x, rows, s, local):
    tokens, d = x.shape
    last = lambda i, t: jnp.minimum(i, jnp.maximum((t[4 + s, local] + (BLOCK - 1)) // BLOCK - 1, 0))
    return pl.pallas_call(
        functools.partial(gather_kernel, s, local),
        grid_spec=pltpu.PrefetchScalarGridSpec(
            num_scalar_prefetch=1,
            grid=(rows // BLOCK,),
            in_specs=[whole(pos), whole(info), whole(x)],
            out_specs=[
                pl.BlockSpec((BLOCK, d), lambda i, t: (last(i, t), 0)),
                pl.BlockSpec((tokens, BLOCK), lambda i, t: (0, last(i, t))),
            ],
        ),
        out_shape=[jax.ShapeDtypeStruct((rows, d), BF16), jax.ShapeDtypeStruct((tokens, rows), BF16)],
        compiler_params=params(),
        cost_estimate=cost(2 * rows * tokens * d, 2 * rows * (tokens + d)),
        name="gather",
    )(table, pos, info, x)


def by_rows(total, most, body):
    for m in range(TILE, most + TILE, TILE):
        pl.when((total > m - TILE) & (total <= m))(functools.partial(body, min(m, most)))


def tiles(total, most, act):
    for t in range(0, most, TILE):
        pl.when(total > t)(functools.partial(act, t, min(TILE, most - t)))


def scatter(table_ref, e, o_ref, out_ref, pad):
    at = 0
    for s in range(4):
        out_ref[s, pl.ds(aligned(table_ref[4 + s, e]), pad), :] = o_ref[pl.ds(aligned(at), pad), :]
        at = at + table_ref[s, e]


def combine(table_ref, local, c_ref, out_ref, acc_ref, ps):
    for s, p in enumerate(ps):
        total = table_ref[4 + s, local]
        blocks = (total + (BLOCK - 1)) // BLOCK

        def clear(k, carry, s=s):
            out_ref[s, pl.ds(aligned(k * GROUP), GROUP), :] = jnp.zeros((GROUP, out_ref.shape[2]), BF16)
            return carry

        lax.fori_loop(total // GROUP, blocks * (BLOCK // GROUP), clear, 0)
        acc_ref[...] = jnp.zeros_like(acc_ref)

        def add(k, carry, s=s):
            at = aligned(k * BLOCK, BLOCK)
            acc_ref[...] += dot(c_ref[s, :, pl.ds(at, BLOCK)], out_ref[s, pl.ds(at, BLOCK), :])
            return carry

        lax.fori_loop(0, blocks, add, 0)
        p[...] = acc_ref[...].astype(p.dtype)


def rows_of(table_ref, e):
    return sum(table_ref[s, e] for s in range(4))


def fetch_c(cs, c_ref, c_sem):
    return [pltpu.make_async_copy(c, c_ref.at[s], c_sem.at[s]) for s, c in enumerate(cs)]


def gate_up_kernel(pad, table_ref, z0, z1, z2, z3, c0, c1, c2, c3, wg_ref, wu_ref, wd_ref, h_hbm, p0, p1, p2, p3,
                   seg_ref, z_ref, h_ref, o_ref, out_ref, c_ref, acc_ref, z_sem, h_sem, c_sem):
    e, local = pl.program_id(0), pl.num_programs(0)
    slot, most = lax.rem(e, 2), z_ref.shape[0]

    def segments(e, slot, start):
        for s, z in enumerate((z0, z1, z2, z3)):
            for k in range(pad // PIECE):

                @pl.when(table_ref[s, e] > k * PIECE)
                def _(s=s, z=z, k=k):
                    at = aligned(table_ref[4 + s, e] + k * PIECE)
                    copy = pltpu.make_async_copy(
                        z.at[pl.ds(at, PIECE)], seg_ref.at[slot, s, pl.ds(k * PIECE, PIECE)], z_sem.at[slot, s, k]
                    )
                    copy.start() if start else copy.wait()

    def put(e, slot, start):
        def act(t, size):
            copy = pltpu.make_async_copy(h_ref.at[slot, pl.ds(t, size)], h_hbm.at[e, pl.ds(t, size)], h_sem.at[slot, t // TILE])
            copy.start() if start else copy.wait()

        tiles(rows_of(table_ref, e), most, act)

    @pl.when(e == 0)
    def _():
        segments(e, slot, True)
        for copy in fetch_c((c0, c1, c2, c3), c_ref, c_sem):
            copy.start()

    @pl.when(e + 1 < local)
    def _():
        segments(e + 1, 1 - slot, True)

    segments(e, slot, False)
    at = 0
    for s in range(4):
        z_ref[pl.ds(aligned(at), pad), :] = seg_ref[slot, s]
        at = at + table_ref[s, e]

    @pl.when(e >= 2)
    def _():
        put(e - 2, slot, False)

    def body(m):
        z = z_ref[:m]
        ff = wg_ref.shape[2]
        half = (ff // 2 + 255) // 256 * 256
        for lo, hi in ((0, half), (half, ff)):
            g = dot(z, wg_ref[0, :, lo:hi])
            u = dot(z, wu_ref[0, :, lo:hi])
            h_ref[slot, :m, lo:hi] = (g * jax.nn.sigmoid(g) * u).astype(BF16)
        o_ref[:m] = dot(h_ref[slot, :m, :], wd_ref[0]).astype(BF16)

    by_rows(at, most, body)
    put(e, slot, True)
    scatter(table_ref, e, o_ref, out_ref, pad)

    @pl.when(e == local - 1)
    def _():
        for copy in fetch_c((c0, c1, c2, c3), c_ref, c_sem):
            copy.wait()
        combine(table_ref, local, c_ref, out_ref, acc_ref, (p0, p1, p2, p3))
        put(e - 1, 1 - slot, False)
        put(e, slot, False)


def partial_sums(tokens, width):
    block = pl.BlockSpec((tokens, width), lambda *_: (0, 0), pipeline_mode=pl.Buffered(1))
    return [block] * 4, [jax.ShapeDtypeStruct((tokens, width), t) for t in (F32, BF16, F32, BF16)]


ANY = pl.BlockSpec(memory_space=pl.ANY)


def gate_up(table, zs, cs, w_gate, w_up, w_down, pad, width):
    (experts, d, ff), (tokens, rows), most = w_gate.shape, cs[0].shape, 4 * pad
    specs, shapes = partial_sums(tokens, width)
    return pl.pallas_call(
        functools.partial(gate_up_kernel, pad),
        grid_spec=pltpu.PrefetchScalarGridSpec(
            num_scalar_prefetch=1,
            grid=(experts,),
            in_specs=[ANY] * 8
            + [pl.BlockSpec((1, d, ff), lambda e, *_: (e, 0, 0))] * 2
            + [pl.BlockSpec((1, ff, width), lambda e, *_: (e, 0, 0))],
            out_specs=[ANY] + specs,
            scratch_shapes=[
                pltpu.VMEM((2, 4, pad, d), BF16),
                pltpu.VMEM((most, d), BF16),
                pltpu.VMEM((2, most, ff), BF16),
                pltpu.VMEM((most, width), BF16),
                pltpu.VMEM((4, rows, width), BF16),
                pltpu.VMEM((4, tokens, rows), BF16),
                pltpu.VMEM((tokens, width), F32),
                pltpu.SemaphoreType.DMA((2, 4, pad // PIECE)),
                pltpu.SemaphoreType.DMA((2, (most + TILE - 1) // TILE)),
                pltpu.SemaphoreType.DMA((4,)),
            ],
        ),
        out_shape=[jax.ShapeDtypeStruct((experts, most, ff), BF16)] + shapes,
        compiler_params=params(),
        cost_estimate=cost(4 * experts * most * d * ff, 4 * experts * d * ff),
        name="gate_up",
    )(table, *zs, *cs, w_gate, w_up, w_down)


def down_kernel(pad, table_ref, h_hbm, w_ref, c0, c1, c2, c3, p0, p1, p2, p3,
                h_ref, o_ref, out_ref, c_ref, acc_ref, h_sem, c_sem):
    e, local = pl.program_id(0), pl.num_programs(0)
    slot, most = lax.rem(e, 2), o_ref.shape[0]

    def get(e, slot, start):
        def act(t, size):
            copy = pltpu.make_async_copy(h_hbm.at[e, pl.ds(t, size)], h_ref.at[slot, pl.ds(t, size)], h_sem.at[slot, t // TILE])
            copy.start() if start else copy.wait()

        tiles(rows_of(table_ref, e), most, act)

    @pl.when(e == 0)
    def _():
        get(e, slot, True)
        for copy in fetch_c((c0, c1, c2, c3), c_ref, c_sem):
            copy.start()

    @pl.when(e + 1 < local)
    def _():
        get(e + 1, 1 - slot, True)

    get(e, slot, False)

    def body(m):
        o_ref[:m] = dot(h_ref[slot, :m, :], w_ref[0]).astype(BF16)

    by_rows(rows_of(table_ref, e), most, body)
    scatter(table_ref, e, o_ref, out_ref, pad)

    @pl.when(e == local - 1)
    def _():
        for copy in fetch_c((c0, c1, c2, c3), c_ref, c_sem):
            copy.wait()
        combine(table_ref, local, c_ref, out_ref, acc_ref, (p0, p1, p2, p3))


def down(table, h, w_down, cs, pad, j, width):
    (experts, ff, d), most, (tokens, rows) = w_down.shape, h.shape[1], cs[0].shape
    specs, shapes = partial_sums(tokens, width)
    return pl.pallas_call(
        functools.partial(down_kernel, pad),
        grid_spec=pltpu.PrefetchScalarGridSpec(
            num_scalar_prefetch=1,
            grid=(experts,),
            in_specs=[ANY, pl.BlockSpec((1, ff, width), lambda e, *_: (e, 0, j))] + [ANY] * 4,
            out_specs=specs,
            scratch_shapes=[
                pltpu.VMEM((2, most, ff), BF16),
                pltpu.VMEM((most, width), BF16),
                pltpu.VMEM((4, rows, width), BF16),
                pltpu.VMEM((4, tokens, rows), BF16),
                pltpu.VMEM((tokens, width), F32),
                pltpu.SemaphoreType.DMA((2, (most + TILE - 1) // TILE)),
                pltpu.SemaphoreType.DMA((4,)),
            ],
        ),
        out_shape=shapes,
        compiler_params=params(),
        cost_estimate=cost(2 * width * (experts * most * ff + 4 * rows * tokens), 2 * experts * width * ff),
        name="down",
    )(table, h, w_down, *cs)


def finish_kernel(p_ref, base_ref, q_ref, back_ref, *refs):
    near = p_ref[...] + base_ref[...] + q_ref[...].astype(F32)
    refs[-1][...] = (near + back_ref[...].astype(F32)).astype(BF16)


def finish(p, base, q, back, y, j):
    (tokens, width), d, tile = p.shape, base.shape[1], 256 if p.shape[0] % 256 == 0 else p.shape[0]
    column = pl.BlockSpec((tile, width), lambda i: (i, j))
    own = pl.BlockSpec((tile, width), lambda i: (i, 0))
    return pl.pallas_call(
        finish_kernel,
        grid=(tokens // tile,),
        in_specs=[own, column, own, own] + ([] if y is None else [ANY]),
        out_specs=column,
        out_shape=jax.ShapeDtypeStruct((tokens, d), BF16),
        input_output_aliases={} if y is None else {4: 0},
        cost_estimate=cost(1e9, 1e6),
        name="finish",
    )(p, base, q, back, *([] if y is None else [y]))


def shared_up_kernel(x_ref, g_ref, u_ref, h_ref):
    g = dot(x_ref[...], g_ref[...])
    u = dot(x_ref[...], u_ref[...])
    h_ref[...] = (g * jax.nn.sigmoid(g) * u).astype(BF16)


def shared_up(x, s_gate, s_up, tile=256):
    (tokens, d), ff = x.shape, s_gate.shape[1]
    return pl.pallas_call(
        shared_up_kernel,
        grid=(ff // tile,),
        in_specs=[whole(x)] + [pl.BlockSpec((d, tile), lambda k: (0, k))] * 2,
        out_specs=pl.BlockSpec((tokens, tile), lambda k: (0, k)),
        out_shape=jax.ShapeDtypeStruct((tokens, ff), BF16),
        compiler_params=params(),
        cost_estimate=cost(4 * tokens * d * ff, 4 * d * ff),
        name="shared_up",
    )(x, s_gate, s_up)


def shared_down_kernel(h_ref, d_ref, y_ref):
    y_ref[...] = dot(h_ref[...], d_ref[...])


def shared_down(h, s_down, tile=512):
    (tokens, ff), d = h.shape, s_down.shape[1]
    return pl.pallas_call(
        shared_down_kernel,
        grid=(d // tile,),
        in_specs=[whole(h), pl.BlockSpec((ff, tile), lambda k: (0, k))],
        out_specs=pl.BlockSpec((tokens, tile), lambda k: (0, k)),
        out_shape=jax.ShapeDtypeStruct((tokens, d), F32),
        compiler_params=params(),
        cost_estimate=cost(2 * tokens * d * ff, 2 * d * ff),
        name="shared_down",
    )(h, s_down)


def solution(mesh):
    members = mesh.shape["ep"]

    def send(v, flip):
        return lax.ppermute(v, "ep", [(i, i ^ flip) for i in range(members)])

    def step(x, expert, slot, gate, w_gate, w_up, w_down, s_gate, s_up, s_down):
        tokens, d = x.shape[2:]
        top, local = expert.shape[3], w_gate.shape[0]
        slots = 5 * tokens * top // (4 * local * members)
        pad = (slots + PIECE - 1) // PIECE * PIECE
        rows = (local * pad + BLOCK - 1) // BLOCK * BLOCK
        x, expert, slot, gate = (v.reshape(v.shape[2:]) for v in (x, expert, slot, gate))
        me = lax.axis_index("ep").astype(I32).reshape(1)

        x2 = send(x, 2)
        code = jnp.where(slot < slots, expert * STRIDE + slot, -1)
        info = jnp.concatenate([code.T.astype(F32), gate.T])
        infos = [info] + [send(info, f) for f in (1, 2, 3)]
        x1 = send(x, 1)
        pos, table = route(me, infos, local, top)
        hs = shared_up(x, s_gate, s_up)
        base = shared_down(hs, s_down)
        zs, cs = [], []
        x3 = send(x2, 1)
        for s, v in enumerate((x, x1, x2, x3)):
            z, c = gather(table, pos, infos[s], v, rows, s, local)
            zs.append(z)
            cs.append(c)
        width, y = d // CHUNKS, None
        h, *ps = gate_up(table, zs, cs, w_gate, w_up, w_down, pad, width)
        parts = []
        for j in range(CHUNKS):
            if j:
                ps = down(table, h, w_down, cs, pad, j, width)
            p0, p1, p2, p3 = ps
            q3 = send(p3, 1)
            back = send((p2 + q3.astype(F32)).astype(BF16), 2)
            q1 = send(p1, 1)
            parts.append((p0, q1, back))
        for j, (p0, q1, back) in enumerate(parts):
            y = finish(p0, base, q1, back, y, j)
        return y.reshape(1, 1, tokens, d)

    data = P("dp", "ep", None, None)
    w, s = P("ep", None, None), P(None, None)
    return jax.shard_map(step, mesh=mesh, in_specs=(data,) * 4 + (w,) * 3 + (s,) * 3, out_specs=data, check_vma=False)
```

time: 1090 us -> 420 us (0.39); the launches traced: 1080 us -> 418 us
  matrix products: 535 us -> 0 us
  Pallas kernels: 0 us -> 263 us
  blocking collectives: 262 us -> 0 us
  local copies, waits for them, and re-layouts: 93 us -> 1.37 us
  waiting for transfers between devices: 175 us -> 103 us
  starting transfers between devices: 8.3 us -> 41.8 us
    dot_general x9 -> x0, matrix products: 535 us -> none  [einsum(): return jnp.einsum(form, a.astype(jnp.float32), b.astype(jnp.float32))]
    pallas_call x0 -> x15, Pallas kernels: none -> 263 us  [the longest x1 89 us: gate_up(): pl.pallas_call(functools.partial(gate_up_kernel, pad), grid_spec=pltpu.Pr...]
    another operation x1 -> x0, blocking collectives: 262 us -> none  [placed(): return lax.with_sharding_constraint(v, NamedSharding(mesh, P(*spec)))]
    another operation x1 -> x0, waiting for transfers between devices: 175 us -> none  [placed(): return lax.with_sharding_constraint(v, NamedSharding(mesh, P(*spec)))]
    ppermute x0 -> x18, waiting for transfers between devices: none -> 103 us  [send(): return lax.ppermute(v, 'ep', [(i, i ^ flip) for i in range(members)])]
    another operation x3 -> x0, local copies, waits for them, and re-layouts: 71 us -> none  [placed(): return lax.with_sharding_constraint(v, NamedSharding(mesh, P(*spec)))]
    ppermute x0 -> x18, starting transfers between devices: none -> 41.8 us  [send(): return lax.ppermute(v, 'ep', [(i, i ^ flip) for i in range(members)])]
    convert_element_type x2 -> x0, local copies, waits for them, and re-layouts: 19.2 us -> none  [the longest x1 17.6 us: step(): einsum('abtke,abtkc->abtec', weighted, to_slot).astype(jnp.bfloat16)]
  transfers between devices with their start and end apart: 1 -> 18, of which waited for: 1 -> 4; matrix products, arithmetic and copies ran while one was open for 8% -> 2% of each run, Pallas kernels for 0% -> 25%
where the time goes in v1:
time: 420 us; the launch traced here: 418 us
  Pallas kernels  263 us (63%)
  waiting for transfers between devices  103 us (25%)
  starting transfers between devices  41.8 us (10%)
  other arithmetic  8.72 us (2%)
    ppermute x18, waiting for transfers between devices, send(): return lax.ppermute(v, 'ep', [(i, i ^ flip) for i in range(members)])  103 us
    pallas_call x1, Pallas kernels, gate_up(): pl.pallas_call(functools.partial(gate_up_kernel, pad), grid_spec=pltpu.Pr...  89 us
    pallas_call x3, Pallas kernels, down(): pl.pallas_call(functools.partial(down_kernel, pad), grid_spec=pltpu.Prefe...  87.2 us
    ppermute x18, starting transfers between devices, send(): return lax.ppermute(v, 'ep', [(i, i ^ flip) for i in range(members)])  41.8 us
    pallas_call x4, Pallas kernels, gather(): pl.pallas_call(functools.partial(gather_kernel, s, local), grid_spec=pltp...  32 us
    pallas_call x1, Pallas kernels, shared_up(): pl.pallas_call(shared_up_kernel, grid=(ff // tile,), in_specs=[whole(x)]...  23.4 us
    pallas_call x4, Pallas kernels, finish(): pl.pallas_call(finish_kernel, grid=(tokens // tile,), in_specs=[own, colu...  15.6 us
    pallas_call x1, Pallas kernels, shared_down(): pl.pallas_call(shared_down_kernel, grid=(d // tile,), in_specs=[whole(h),...  13.9 us
  transfers between devices with their start and end apart: 18, of which 4 were waited for; matrix products, arithmetic and copies ran while one was open for 2% of the time, Pallas kernels for 25%

profile of v1, /device:TPU:0, one launch (start us, length us, event | category | flops | bytes accessed | tf_op | source)
XLA Modules:
  0.0 418.4 jit_solution(16015643991721255018)
XLA Ops:
  0.0 3.3 collective-permute-start.4
  4.8 66.9 %collective-permute-done.4.x_ref = bf16[768,2048]{1,0:T(8,128)(2,1)} collective-permute-done((bf16[768,2048]{1,0:T(8,128)(2,1)}, bf16[768,2048]{1,0:T(8,128)(2,1)}, u32[]{:S(2)}, u32[]{:S(2)}) %collective-permute-start.4) | collective-permute-done | bytes 3145760 | tf_op jit(solution)/shard_map/ppermute | solution.py:391
  74.0 23.4 %shared_up.1.h_ref = bf16[768,2816]{1,0:T(8,128)(2,1)} custom-call(bf16[768,2048]{1,0:T(8,128)(2,1)} %bitcast.15, bf16[2048,2816]{1,0:T(8,128)(2,1)} %g_ref.1, bf16[2048,2816]{1,0:T(8,128)(2,1)} %u_ref.1), custom_call_target="tpu_custom_call" | custom-call | flops 17716740096 | bytes 23068672 | tf_op jit(solution)/shard_map/shared_up/pallas_call | solution.py:357
  98.1 2.3 route.1
  100.4 8.0 %gather.4 = (bf16[1536,2048]{1,0:T(8,128)(2,1)}, bf16[768,1536]{1,0:T(8,128)(2,1)}) custom-call(s32[8,128]{1,0:T(8,128)} %get-tuple-element.32.table_ref, s32[4,6,768]{2,1,0:T(8,128)} %get-tuple-element.33.pos_ref, f32[12,768]{1,0:T(8,128)} %copy-done.5, bf16[768,2048]{1,0:T(8,128)(2,1)} %bitcast.16), custom_call_target="tpu_custom_call" | custom-call | flops 4831838208 | bytes 8650752 | tf_op jit(solution)/shard_map/gather/pallas_call | solution.py:93
  108.3 8.0 %gather.6 = (bf16[1536,2048]{1,0:T(8,128)(2,1)}, bf16[768,1536]{1,0:T(8,128)(2,1)}) custom-call(s32[8,128]{1,0:T(8,128)} %get-tuple-element.32.table_ref, s32[4,6,768]{2,1,0:T(8,128)} %get-tuple-element.33.pos_ref, f32[12,768]{1,0:T(8,128)} %copy-done.8, bf16[768,2048]{1,0:T(8,128)(2,1)} %collective-permute-done.4.x_ref), custom_call_target="tpu_custom_call" | custom-call | flops 4831838208 | bytes 8650752 | tf_op jit(solution)/shard_map/gather/pallas_call | solution.py:93
  116.4 8.0 %gather.5 = (bf16[1536,2048]{1,0:T(8,128)(2,1)}, bf16[768,1536]{1,0:T(8,128)(2,1)}) custom-call(s32[8,128]{1,0:T(8,128)} %get-tuple-element.32.table_ref, s32[4,6,768]{2,1,0:T(8,128)} %get-tuple-element.33.pos_ref, f32[12,768]{1,0:T(8,128)} %copy-done.7, bf16[768,2048]{1,0:T(8,128)(2,1)} %collective-permute-done.3.x_ref), custom_call_target="tpu_custom_call" | custom-call | flops 4831838208 | bytes 8650752 | tf_op jit(solution)/shard_map/gather/pallas_call | solution.py:93
  124.4 8.0 %gather.7 = (bf16[1536,2048]{1,0:T(8,128)(2,1)}, bf16[768,1536]{1,0:T(8,128)(2,1)}) custom-call(s32[8,128]{1,0:T(8,128)} %get-tuple-element.32.table_ref, s32[4,6,768]{2,1,0:T(8,128)} %get-tuple-element.33.pos_ref, f32[12,768]{1,0:T(8,128)} %copy-done.6, bf16[768,2048]{1,0:T(8,128)(2,1)} %collective-permute-done.5.x_ref), custom_call_target="tpu_custom_call" | custom-call | flops 4831838208 | bytes 8650752 | tf_op jit(solution)/shard_map/gather/pallas_call | solution.py:93
  132.4 89.0 %gate_up.1 = (bf16[16,384,1408]{2,1,0:T(8,128)(2,1)}, f32[768,512]{1,0:T(8,128)}, bf16[768,512]{1,0:T(8,128)(2,1)}, f32[768,512]{1,0:T(8,128)}, bf16[768,512]{1,0:T(8,128)(2,1)}) custom-call(s32[8,128]{1,0:T(8,128)} %get-tuple-element.32.table_ref, bf16[1536,2048]{1,0:T(8,128)(2,1)} %get-tuple-element.34.z0, bf16[1536,2048]{1,0:T(8,128)(2,1)} %get-tuple-element.35.z1, ...), custom_call_target="tpu_custom_call" | custom-call | flops 70866960384 | bytes 184549376 | tf_op jit(solution)/shard_map/gate_up/pallas_call | solution.py:235
  221.4 29.2 %down.5 = (f32[768,512]{1,0:T(8,128)}, bf16[768,512]{1,0:T(8,128)(2,1)}, f32[768,512]{1,0:T(8,128)}, bf16[768,512]{1,0:T(8,128)(2,1)}) custom-call(s32[8,128]{1,0:T(8,128)} %get-tuple-element.32.table_ref, bf16[16,384,1408]{2,1,0:T(8,128)(2,1)} %get-tuple-element.42.h_hbm, bf16[16,1408,2048]{2,1,0:T(8,128)(2,1)} %w_ref.5, ...), custom_call_target="tpu_custom_call" | custom-call | flops 13690208256 | bytes 23068672 | tf_op jit(solution)/shard_map/down/pallas_call | solution.py:304
  250.6 29.0 %down.4 = (f32[768,512]{1,0:T(8,128)}, bf16[768,512]{1,0:T(8,128)(2,1)}, f32[768,512]{1,0:T(8,128)}, bf16[768,512]{1,0:T(8,128)(2,1)}) custom-call(s32[8,128]{1,0:T(8,128)} %get-tuple-element.32.table_ref, bf16[16,384,1408]{2,1,0:T(8,128)(2,1)} %get-tuple-element.42.h_hbm, bf16[16,1408,2048]{2,1,0:T(8,128)(2,1)} %w_ref.5, ...), custom_call_target="tpu_custom_call" | custom-call | flops 13690208256 | bytes 23068672 | tf_op jit(solution)/shard_map/down/pallas_call | solution.py:304
  279.6 29.5 %collective-permute-start.16 = (bf16[768,512]{1,0:T(8,128)(2,1)}, bf16[768,512]{1,0:T(8,128)(2,1)}, u32[]{:S(2)}, u32[]{:S(2)}) collective-permute-start(bf16[768,512]{1,0:T(8,128)(2,1)} %get-tuple-element.58), channel_id=1, source_target_pairs={{0,1},{1,0},{2,3},{3,2},{4,5},{5,4},{6,7},{7,6}} | collective-permute-start | bytes 2359304 | tf_op jit(solution)/shard_map/ppermute | solution.py:391
  309.7 29.0 %down.3 = (f32[768,512]{1,0:T(8,128)}, bf16[768,512]{1,0:T(8,128)(2,1)}, f32[768,512]{1,0:T(8,128)}, bf16[768,512]{1,0:T(8,128)(2,1)}) custom-call(s32[8,128]{1,0:T(8,128)} %get-tuple-element.32.table_ref, bf16[16,384,1408]{2,1,0:T(8,128)(2,1)} %get-tuple-element.42.h_hbm, bf16[16,1408,2048]{2,1,0:T(8,128)(2,1)} %w_ref.5, ...), custom_call_target="tpu_custom_call" | custom-call | flops 13690208256 | bytes 23068672 | tf_op jit(solution)/shard_map/down/pallas_call | solution.py:304
  338.7 3.2 collective-permute-start.15
  344.3 2.4 add_convert_fusion.1
  346.8 2.5 add_convert_fusion.2
  352.9 11.9 %collective-permute-done.17.back_ref = bf16[768,512]{1,0:T(8,128)(2,1)} collective-permute-done((bf16[768,512]{1,0:T(8,128)(2,1)S(1)}, bf16[768,512]{1,0:T(8,128)(2,1)}, u32[]{:S(2)}, u32[]{:S(2)}) %collective-permute-start.17) | collective-permute-done | bytes 786464 | tf_op jit(solution)/shard_map/ppermute | solution.py:391
  364.8 13.9 %shared_down.1.base_ref = f32[768,2048]{1,0:T(8,128)} custom-call(bf16[768,2816]{1,0:T(8,128)(2,1)} %shared_up.1.h_ref, bf16[2816,2048]{1,0:T(8,128)(2,1)} %d_ref.1), custom_call_target="tpu_custom_call" | custom-call | flops 8858370048 | bytes 11534336 | tf_op jit(solution)/shard_map/shared_down/pallas_call | solution.py:375
  378.8 3.9 finish.4.refs_0_
  382.7 3.9 finish.5.refs_0_
  386.6 12.0 %collective-permute-done.11.back_ref = bf16[768,512]{1,0:T(8,128)(2,1)} collective-permute-done((bf16[768,512]{1,0:T(8,128)(2,1)}, bf16[768,512]{1,0:T(8,128)(2,1)}, u32[]{:S(2)}, u32[]{:S(2)}) %collective-permute-start.11) | collective-permute-done | bytes 786464 | tf_op jit(solution)/shard_map/ppermute | solution.py:391
  398.5 3.9 finish.6.refs_0_
  402.4 12.0 %collective-permute-done.8.back_ref = bf16[768,512]{1,0:T(8,128)(2,1)} collective-permute-done((bf16[768,512]{1,0:T(8,128)(2,1)}, bf16[768,512]{1,0:T(8,128)(2,1)}, u32[]{:S(2)}, u32[]{:S(2)}) %collective-permute-start.8) | collective-permute-done | bytes 786464 | tf_op jit(solution)/shard_map/ppermute | solution.py:391
  414.5 3.9 finish.7
  (52 shorter events, 11.0 us)
Async XLA Ops:
  0.0 71.7 %collective-permute-start.4 = (bf16[768,2048]{1,0:T(8,128)(2,1)}, bf16[768,2048]{1,0:T(8,128)(2,1)}, u32[]{:S(2)}, u32[]{:S(2)}) collective-permute-start(bf16[768,2048]{1,0:T(8,128)(2,1)} %bitcast.13), channel_id=1, source_target_pairs={{0,2},{1,3},{2,0},{3,1},{4,6},{5,7},{6,4},{7,5}} | collective-permute-start | bytes 9437192 | tf_op jit(solution)/shard_map/ppermute | solution.py:391
  3.3 113.1 %collective-permute-start.3 = (bf16[768,2048]{1,0:T(8,128)(2,1)}, bf16[768,2048]{1,0:T(8,128)(2,1)}, u32[]{:S(2)}, u32[]{:S(2)}) collective-permute-start(bf16[768,2048]{1,0:T(8,128)(2,1)} %bitcast.14), channel_id=1, source_target_pairs={{0,1},{1,0},{2,3},{3,2},{4,5},{5,4},{6,7},{7,6}} | collective-permute-start | bytes 9437192 | tf_op jit(solution)/shard_map/ppermute | solution.py:391
  71.7 52.7 %collective-permute-start.5 = (bf16[768,2048]{1,0:T(8,128)(2,1)}, bf16[768,2048]{1,0:T(8,128)(2,1)}, u32[]{:S(2)}, u32[]{:S(2)}) collective-permute-start(bf16[768,2048]{1,0:T(8,128)(2,1)} %collective-permute-done.4.x_ref), channel_id=1, source_target_pairs={{0,1},{1,0},{2,3},{3,2},{4,5},{5,4},{6,7},{7,6}} | collective-permute-start | bytes 9437192 | tf_op jit(solution)/shard_map/ppermute | solution.py:391
  71.7 25.7 %copy-start.5 = (f32[12,768]{1,0:T(8,128)}, f32[12,768]{1,0:T(8,128)S(1)}, u32[]{:S(2)}) copy-start(f32[12,768]{1,0:T(8,128)S(1)} %pad_maximum_fusion.refs_0_.info_ref) | copy-start | bytes 110596
  71.8 25.7 %collective-permute-start = (f32[12,768]{1,0:T(8,128)S(1)}, f32[12,768]{1,0:T(8,128)S(1)}, u32[]{:S(2)}, u32[]{:S(2)}) collective-permute-start(f32[12,768]{1,0:T(8,128)S(1)} %pad_maximum_fusion.refs_0_.info_ref), channel_id=1, source_target_pairs={{0,1},{1,0},{2,3},{3,2},{4,5},{5,4},{6,7},{7,6}} | collective-permute-start | bytes 110600 | tf_op jit(solution)/shard_map/ppermute | solution.py:391
  72.3 25.2 %collective-permute-start.1 = (f32[12,768]{1,0:T(8,128)S(1)}, f32[12,768]{1,0:T(8,128)S(1)}, u32[]{:S(2)}, u32[]{:S(2)}) collective-permute-start(f32[12,768]{1,0:T(8,128)S(1)} %pad_maximum_fusion.refs_0_.info_ref), channel_id=1, source_target_pairs={{0,2},{1,3},{2,0},{3,1},{4,6},{5,7},{6,4},{7,5}} | collective-permute-start | bytes 110600 | tf_op jit(solution)/shard_map/ppermute | solution.py:391
  74.0 23.4 %collective-permute-start.2 = (f32[12,768]{1,0:T(8,128)S(1)}, f32[12,768]{1,0:T(8,128)S(1)}, u32[]{:S(2)}, u32[]{:S(2)}) collective-permute-start(f32[12,768]{1,0:T(8,128)S(1)} %pad_maximum_fusion.refs_0_.info_ref), channel_id=1, source_target_pairs={{0,3},{1,2},{2,1},{3,0},{4,7},{5,6},{6,5},{7,4}} | collective-permute-start | bytes 110600 | tf_op jit(solution)/shard_map/ppermute | solution.py:391
  279.6 62.3 %collective-permute-start.16 = (bf16[768,512]{1,0:T(8,128)(2,1)}, bf16[768,512]{1,0:T(8,128)(2,1)}, u32[]{:S(2)}, u32[]{:S(2)}) collective-permute-start(bf16[768,512]{1,0:T(8,128)(2,1)} %get-tuple-element.58), channel_id=1, source_target_pairs={{0,1},{1,0},{2,3},{3,2},{4,5},{5,4},{6,7},{7,6}} | collective-permute-start | bytes 2359304 | tf_op jit(solution)/shard_map/ppermute | solution.py:391
  309.1 35.1 %collective-permute-start.13 = (bf16[768,512]{1,0:T(8,128)(2,1)}, bf16[768,512]{1,0:T(8,128)(2,1)}, u32[]{:S(2)}, u32[]{:S(2)}) collective-permute-start(bf16[768,512]{1,0:T(8,128)(2,1)} %get-tuple-element.54), channel_id=1, source_target_pairs={{0,1},{1,0},{2,3},{3,2},{4,5},{5,4},{6,7},{7,6}} | collective-permute-start | bytes 2359304 | tf_op jit(solution)/shard_map/ppermute | solution.py:391
  309.2 37.6 %collective-permute-start.10 = (bf16[768,512]{1,0:T(8,128)(2,1)}, bf16[768,512]{1,0:T(8,128)(2,1)}, u32[]{:S(2)}, u32[]{:S(2)}) collective-permute-start(bf16[768,512]{1,0:T(8,128)(2,1)} %get-tuple-element.50), channel_id=1, source_target_pairs={{0,1},{1,0},{2,3},{3,2},{4,5},{5,4},{6,7},{7,6}} | collective-permute-start | bytes 2359304 | tf_op jit(solution)/shard_map/ppermute | solution.py:391
  338.7 5.6 %copy-start.1 = (f32[768,512]{1,0:T(8,128)S(1)}, f32[768,512]{1,0:T(8,128)}, u32[]{:S(2)}) copy-start(f32[768,512]{1,0:T(8,128)} %get-tuple-element.53) | copy-start | bytes 4718596
  338.7 12.2 %collective-permute-start.15 = (bf16[768,512]{1,0:T(8,128)(2,1)}, bf16[768,512]{1,0:T(8,128)(2,1)S(1)}, u32[]{:S(2)}, u32[]{:S(2)}) collective-permute-start(bf16[768,512]{1,0:T(8,128)(2,1)} %get-tuple-element.56), channel_id=1, source_target_pairs={{0,1},{1,0},{2,3},{3,2},{4,5},{5,4},{6,7},{7,6}} | collective-permute-start | bytes 2359304 | tf_op jit(solution)/shard_map/ppermute | solution.py:391
  341.9 10.9 %collective-permute-start.12 = (bf16[768,512]{1,0:T(8,128)(2,1)}, bf16[768,512]{1,0:T(8,128)(2,1)S(1)}, u32[]{:S(2)}, u32[]{:S(2)}) collective-permute-start(bf16[768,512]{1,0:T(8,128)(2,1)} %get-tuple-element.52), channel_id=1, source_target_pairs={{0,1},{1,0},{2,3},{3,2},{4,5},{5,4},{6,7},{7,6}} | collective-permute-start | bytes 2359304 | tf_op jit(solution)/shard_map/ppermute | solution.py:391
  341.9 7.4 %collective-permute-start.7 = (bf16[768,512]{1,0:T(8,128)(2,1)}, bf16[768,512]{1,0:T(8,128)(2,1)S(1)}, u32[]{:S(2)}, u32[]{:S(2)}) collective-permute-start(bf16[768,512]{1,0:T(8,128)(2,1)} %get-tuple-element.46), channel_id=1, source_target_pairs={{0,1},{1,0},{2,3},{3,2},{4,5},{5,4},{6,7},{7,6}} | collective-permute-start | bytes 2359304 | tf_op jit(solution)/shard_map/ppermute | solution.py:391
  344.3 2.5 copy-start
  344.3 20.5 %collective-permute-start.17 = (bf16[768,512]{1,0:T(8,128)(2,1)S(1)}, bf16[768,512]{1,0:T(8,128)(2,1)}, u32[]{:S(2)}, u32[]{:S(2)}) collective-permute-start(bf16[768,512]{1,0:T(8,128)(2,1)S(1)} %add_convert_fusion), channel_id=1, source_target_pairs={{0,2},{1,3},{2,0},{3,1},{4,6},{5,7},{6,4},{7,5}} | collective-permute-start | bytes 2359304 | tf_op jit(solution)/shard_map/ppermute | solution.py:391
  346.8 2.9 copy-start.2
  346.8 39.8 %collective-permute-start.9 = (bf16[768,512]{1,0:T(8,128)(2,1)}, bf16[768,512]{1,0:T(8,128)(2,1)}, u32[]{:S(2)}, u32[]{:S(2)}) collective-permute-start(bf16[768,512]{1,0:T(8,128)(2,1)} %get-tuple-element.48), channel_id=1, source_target_pairs={{0,1},{1,0},{2,3},{3,2},{4,5},{5,4},{6,7},{7,6}} | collective-permute-start | bytes 2359304 | tf_op jit(solution)/shard_map/ppermute | solution.py:391
  349.3 53.1 %collective-permute-start.6 = (bf16[768,512]{1,0:T(8,128)(2,1)}, bf16[768,512]{1,0:T(8,128)(2,1)}, u32[]{:S(2)}, u32[]{:S(2)}) collective-permute-start(bf16[768,512]{1,0:T(8,128)(2,1)} %get-tuple-element.44), channel_id=1, source_target_pairs={{0,1},{1,0},{2,3},{3,2},{4,5},{5,4},{6,7},{7,6}} | collective-permute-start | bytes 2359304 | tf_op jit(solution)/shard_map/ppermute | solution.py:391
  350.9 27.9 %copy-start.3 = (bf16[768,512]{1,0:T(8,128)(2,1)}, bf16[768,512]{1,0:T(8,128)(2,1)S(1)}, u32[]{:S(2)}) copy-start(bf16[768,512]{1,0:T(8,128)(2,1)S(1)} %collective-permute-done.15.q_ref) | copy-start | bytes 2359300
  350.9 31.8 %collective-permute-start.14 = (bf16[768,512]{1,0:T(8,128)(2,1)}, bf16[768,512]{1,0:T(8,128)(2,1)}, u32[]{:S(2)}, u32[]{:S(2)}) collective-permute-start(bf16[768,512]{1,0:T(8,128)(2,1)} %add_convert_fusion.1), channel_id=1, source_target_pairs={{0,2},{1,3},{2,0},{3,1},{4,6},{5,7},{6,4},{7,5}} | collective-permute-start | bytes 2359304 | tf_op jit(solution)/shard_map/ppermute | solution.py:391
  352.8 12.1 %copy-start.4 = (bf16[768,512]{1,0:T(8,128)(2,1)}, bf16[768,512]{1,0:T(8,128)(2,1)S(1)}, u32[]{:S(2)}) copy-start(bf16[768,512]{1,0:T(8,128)(2,1)S(1)} %collective-permute-done.12.q_ref) | copy-start | bytes 2359300
  352.8 45.8 %collective-permute-start.11 = (bf16[768,512]{1,0:T(8,128)(2,1)}, bf16[768,512]{1,0:T(8,128)(2,1)}, u32[]{:S(2)}, u32[]{:S(2)}) collective-permute-start(bf16[768,512]{1,0:T(8,128)(2,1)} %add_convert_fusion.2), channel_id=1, source_target_pairs={{0,2},{1,3},{2,0},{3,1},{4,6},{5,7},{6,4},{7,5}} | collective-permute-start | bytes 2359304 | tf_op jit(solution)/shard_map/ppermute | solution.py:391
  364.8 49.6 %collective-permute-start.8 = (bf16[768,512]{1,0:T(8,128)(2,1)}, bf16[768,512]{1,0:T(8,128)(2,1)}, u32[]{:S(2)}, u32[]{:S(2)}) collective-permute-start(bf16[768,512]{1,0:T(8,128)(2,1)} %add_convert_fusion.3), channel_id=1, source_target_pairs={{0,2},{1,3},{2,0},{3,1},{4,6},{5,7},{6,4},{7,5}} | collective-permute-start | bytes 2359304 | tf_op jit(solution)/shard_map/ppermute | solution.py:391
  (3 other events, 1.9 us)
